TPU v7x, 8 devices: a whole 2x2x1 slice. The times are simulated.
8 devices in a mesh: replica: 2 (over z, y), stage: 4 (over x, core).
Axes of the slice: x: 2, y: 2, z: 1, core: 2. Of those that a mesh axis runs over, the one named last changes fastest.
Arguments:
- embeddings: bfloat16 [8192, 3072], P('replica'), parts along dimension 0
- valid_len: int32 [2], P('replica'), parts along dimension 0
- attn_gain: float32 [4, 3072], P('stage')
- w_q: bfloat16 [4, 3072, 24, 128], P('stage')
- w_k: bfloat16 [4, 3072, 8, 128], P('stage')
- w_v: bfloat16 [4, 3072, 8, 128], P('stage')
- w_o: bfloat16 [4, 24, 128, 3072], P('stage')
- mlp_gain: float32 [4, 3072], P('stage')
- w_gate: bfloat16 [4, 3072, 8192], P('stage')
- w_up: bfloat16 [4, 3072, 8192], P('stage')
- w_down: bfloat16 [4, 8192, 3072], P('stage')
Outputs:
- output 1: bfloat16 [8192, 3072], P(('replica', 'stage')), parts along dimension 0
- output 2: bfloat16 [4, 8192, 8, 128], P('stage', 'replica'), parts along dimension 1
- output 3: bfloat16 [4, 8192, 8, 128], P('stage', 'replica'), parts along dimension 1
There are 2 independent parts. A program takes and returns all parts, laid end to end along the dimension named above; an argument that names none is the same for every part.
All inputs are finite; a program needn't handle non-finite values.
Results may differ from a plain program's by a relative error of at most 0.02.
Values are sent between devices in bfloat16 or wider.
A program may use at most 1 GiB of HBM per device.

v0:
```python
import jax
import jax.numpy as jnp
from jax import lax
from jax.sharding import PartitionSpec as P

EPS = 1e-5
ROPE_BASE = 10000.0
NEG_BIG = -1e30


def rms_norm(hidden, norm_gain):
    hid32 = hidden.astype(jnp.float32)
    inv_rms = lax.rsqrt(jnp.mean(hid32 * hid32, axis=-1, keepdims=True) + EPS)
    return (hid32 * inv_rms * norm_gain).astype(jnp.bfloat16)


def rope_tables(positions, head_dim):
    half_dim = head_dim // 2
    inv_freq = ROPE_BASE ** (-jnp.arange(half_dim, dtype=jnp.float32) * (2.0 / head_dim))
    angles = positions.astype(jnp.float32)[:, None] * inv_freq[None, :]
    return jnp.cos(angles), jnp.sin(angles)


def apply_rope(values, cos_tab, sin_tab):
    half_dim = values.shape[-1] // 2
    front_half = values[..., :half_dim]
    back_half = values[..., half_dim:]
    return jnp.concatenate([front_half * cos_tab - back_half * sin_tab, back_half * cos_tab + front_half * sin_tab], axis=-1)


def project_qkv(normed, layer_idx, params, positions):
    w_q, w_k, w_v = params[1], params[2], params[3]
    d_model, kv_heads, head_dim = w_k.shape[1], w_k.shape[2], w_k.shape[3]
    group_size = w_q.shape[2] // kv_heads
    w_q_heads = w_q[layer_idx].reshape(d_model, kv_heads, group_size, head_dim)
    q_proj = jnp.einsum('sd,dhgk->shgk', normed, w_q_heads, preferred_element_type=jnp.float32)
    k_proj = jnp.einsum('sd,dhk->shk', normed, w_k[layer_idx], preferred_element_type=jnp.float32)
    v_new = jnp.einsum('sd,dhk->shk', normed, w_v[layer_idx], preferred_element_type=jnp.float32).astype(jnp.bfloat16)
    cos_tab, sin_tab = rope_tables(positions, head_dim)
    q_rot = apply_rope(q_proj, cos_tab[:, None, None, :], sin_tab[:, None, None, :]).astype(jnp.bfloat16)
    k_rot = apply_rope(k_proj, cos_tab[:, None, :], sin_tab[:, None, :]).astype(jnp.bfloat16)
    return q_rot, k_rot, v_new


def causal_attention(q_block, key_all, value_all, q_start, n_key_blocks, valid_pos):
    block_len, kv_heads, group_size, head_dim = q_block.shape
    score_scale = head_dim ** -0.5
    q_pos = q_start + jnp.arange(block_len)

    def key_step(block_idx, loop_state):
        run_max, run_sum, acc_out = loop_state
        k_start = block_idx * block_len
        key_blk = lax.dynamic_slice_in_dim(key_all, k_start, block_len, axis=0)
        value_blk = lax.dynamic_slice_in_dim(value_all, k_start, block_len, axis=0)
        scores = jnp.einsum('qhgd,khd->hgqk', q_block, key_blk, preferred_element_type=jnp.float32) * score_scale
        k_pos = k_start + jnp.arange(block_len)
        allowed = (k_pos[None, :] <= q_pos[:, None]) & (k_pos[None, :] < valid_pos)
        scores = jnp.where(allowed, scores, NEG_BIG)
        new_max = jnp.maximum(run_max, jnp.max(scores, axis=-1))
        rescale = jnp.exp(run_max - new_max)
        probs_blk = jnp.exp(scores - new_max[..., None])
        run_sum = run_sum * rescale + jnp.sum(probs_blk, axis=-1)
        acc_out = acc_out * rescale[..., None] + jnp.einsum('hgqk,khd->hgqd', probs_blk.astype(jnp.bfloat16), value_blk, preferred_element_type=jnp.float32)
        return new_max, run_sum, acc_out

    init_state = (jnp.full((kv_heads, group_size, block_len), NEG_BIG, jnp.float32),
                  jnp.zeros((kv_heads, group_size, block_len), jnp.float32),
                  jnp.zeros((kv_heads, group_size, block_len, head_dim), jnp.float32))
    run_max, run_sum, acc_out = lax.fori_loop(0, n_key_blocks, key_step, init_state)
    return (acc_out / run_sum[..., None]).astype(jnp.bfloat16)


def mlp_block(hidden, attn_out, layer_idx, params):
    mlp_gain, w_gate, w_up, w_down = params[5], params[6], params[7], params[8]
    hidden = (hidden.astype(jnp.float32) + attn_out).astype(jnp.bfloat16)
    normed = rms_norm(hidden, mlp_gain[layer_idx])
    gate_proj = jnp.dot(normed, w_gate[layer_idx], preferred_element_type=jnp.float32)
    up_proj = jnp.dot(normed, w_up[layer_idx], preferred_element_type=jnp.float32)
    act_val = (jax.nn.silu(gate_proj) * up_proj).astype(jnp.bfloat16)
    down_proj = jnp.dot(act_val, w_down[layer_idx], preferred_element_type=jnp.float32)
    return (hidden.astype(jnp.float32) + down_proj).astype(jnp.bfloat16)


def block_layer(hidden, layer_idx, params, key_cache, value_cache, blk_index, valid_pos):
    block_len = hidden.shape[0]
    q_start = blk_index * block_len
    normed = rms_norm(hidden, params[0][layer_idx])
    q_rot, k_rot, v_new = project_qkv(normed, layer_idx, params, q_start + jnp.arange(block_len))
    key_cache = lax.dynamic_update_slice(key_cache, k_rot[None], (layer_idx, q_start, 0, 0))
    value_cache = lax.dynamic_update_slice(value_cache, v_new[None], (layer_idx, q_start, 0, 0))
    attn_heads = causal_attention(q_rot, key_cache[layer_idx], value_cache[layer_idx], q_start, blk_index + 1, valid_pos)
    kv_heads, group_size, head_dim = attn_heads.shape[0], attn_heads.shape[1], attn_heads.shape[3]
    w_o_heads = params[4][layer_idx].reshape(kv_heads, group_size, head_dim, -1)
    attn_out = jnp.einsum('hgqd,hgde->qe', attn_heads, w_o_heads, preferred_element_type=jnp.float32)
    return mlp_block(hidden, attn_out, layer_idx, params), key_cache, value_cache


def solution(mesh):
    stages = mesh.shape['stage']
    send_pairs = [(src_stage, src_stage + 1) for src_stage in range(stages - 1)]
    gain_spec = P('stage', None)
    spec_three = P('stage', None, None)
    spec_four = P('stage', None, None, None)

    def stage_program(embeddings, valid_len, attn_gain, w_q, w_k, w_v, w_o, mlp_gain, w_gate, w_up, w_down):
        params = (attn_gain, w_q, w_k, w_v, w_o, mlp_gain, w_gate, w_up, w_down)
        seq_len, d_model = embeddings.shape
        block_len = seq_len // stages
        layers_here = w_q.shape[0]
        cache_shape = (layers_here, seq_len, w_k.shape[2], w_k.shape[3])
        my_stage = lax.axis_index('stage')
        valid_pos = valid_len[0]

        def run_stage(operands):
            hidden, key_cache, value_cache, blk_index = operands
            for layer_idx in range(layers_here):
                hidden, key_cache, value_cache = block_layer(hidden, layer_idx, params, key_cache, value_cache, blk_index, valid_pos)
            return hidden, key_cache, value_cache

        def skip_stage(operands):
            return operands[0], operands[1], operands[2]

        def tick_fn(tick_idx, loop_state):
            recv_buf, key_cache, value_cache, out_blocks = loop_state
            blk_index = tick_idx - my_stage
            active = (blk_index >= 0) & (blk_index < stages)
            blk_index = jnp.clip(blk_index, 0, stages - 1)
            own_block = lax.dynamic_slice_in_dim(embeddings, blk_index * block_len, block_len, axis=0)
            hidden_in = jnp.where(my_stage == 0, own_block, recv_buf)
            hidden_out, key_cache, value_cache = lax.cond(active, run_stage, skip_stage, (hidden_in, key_cache, value_cache, blk_index))
            out_blocks = lax.cond(active & (my_stage == stages - 1),
                                  lambda blocks: lax.dynamic_update_slice(blocks, hidden_out[None], (blk_index, 0, 0)),
                                  lambda blocks: blocks, out_blocks)
            recv_buf = lax.ppermute(hidden_out, 'stage', send_pairs)
            return recv_buf, key_cache, value_cache, out_blocks

        init_state = (jnp.zeros((block_len, d_model), jnp.bfloat16),
                      jnp.zeros(cache_shape, jnp.bfloat16),
                      jnp.zeros(cache_shape, jnp.bfloat16),
                      jnp.zeros((stages, block_len, d_model), jnp.bfloat16))
        recv_buf, key_cache, value_cache, out_blocks = lax.fori_loop(0, 2 * stages - 1, tick_fn, init_state)
        delivered = lax.all_to_all(out_blocks, 'stage', 0, 0, tiled=True)
        return delivered[stages - 1], key_cache, value_cache

    return jax.shard_map(stage_program, mesh=mesh,
                         in_specs=(P('replica', None), P('replica'), gain_spec, spec_four, spec_four, spec_four, spec_four,
                                   gain_spec, spec_three, spec_three, spec_three),
                         out_specs=(P(('replica', 'stage'), None), P('stage', 'replica', None, None), P('stage', 'replica', None, None)),
                         check_vma=False)
```

profile of v0, /device:TPU:5, one launch (start us, length us, event | category | flops | bytes accessed | tf_op | source)
XLA Modules:
  0.0 5160.5 jit_solution(12838656187921894030)
XLA Ops:
  60.8 4178.4 %while.38 = (s32[]{:T(128)}, bf16[1024,3072]{1,0:T(8,128)(2,1)}, bf16[1,4096,8,128]{3,1,2,0:T(8,128)(2,1)}, bf16[1,4096,8,128]{3,1,2,0:T(8,128)(2,1)}, bf16[4,10...) while((s32[]{:T(128)}, bf16[1024,3072]{1,0:T(8,128)(2,1)}, ...), condition=%wide.region_11.12_spmd, body=%wide.region_0.11_spmd.sunk | while | flops 219523710976 | bytes 945245696 | solution.py:141
  76.4 416.0 %collective-permute-done = bf16[1024,3072]{1,0:T(8,128)(2,1)} collective-permute-done((bf16[1024,3072]{1,0:T(8,128)(2,1)}, bf16[1024,3072]{1,0:T(8,128)(2,1)}, u32[]{:S(2)}, u32[]{:S(2)}) %collective-permute-start) | collective-permute-done | bytes 6291488 | tf_op jit(solution)/shard_map/while/body/eval_jaxpr/ppermute | solution.py:134
  502.6 411.4 %conditional.4 = ((bf16[1024,3072]{1,0:T(8,128)(2,1)}, bf16[1,4096,8,128]{3,1,2,0:T(8,128)(2,1)}, bf16[1,4096,8,128]{3,1,2,0:T(8,128)(2,1)})) conditional(s32[]{:T(128)} %convert_element_type.145, (bf16[1024,3072]{1,0:T(8,128)(2,1)}, bf16[1,4096,8,128]{3,1,2,0:T(8,128)(2,1)}, bf16[1,4096,8,128]{3,1,2,0:T(8,128)(2,1)}) %tuple.85, ...), branch_computations={%region_1.1_spmd, %region_2.8_spmd} | conditional | flops 219520565248 | bytes 888622080 | solution.py:130
  584.0 115.0 %while.37 = (s32[]{:T(128)}, f32[8,3,1024]{2,1,0:T(4,128)S(1)}, f32[8,3,1024]{2,1,0:T(4,128)S(1)}, f32[8,3,1024,128]{3,2,1,0:T(8,128)}, s32[]{:T(128)}, /*index=...) while((s32[]{:T(128)}, f32[8,3,1024]{2,1,0:T(4,128)S(1)}, ...), condition=%wide.region_7.6_spmd.clone, body=%wide.region_4.5_spmd.clone.sunk | while | flops 13170167808 | bytes 343427264 | solution.py:69
  729.1 60.3 %fusion.23 = f32[1024,8192]{1,0:T(8,128)} fusion(bf16[1,3072,8192]{2,1,0:T(8,128)(2,1)} %get-tuple-element.449, bf16[1024,3072]{1,0:T(8,128)(2,1)} %get-tuple-element.614, f32[3072]{0:T(1024)S(1)} %bitcast.123, f32[1024]{0:T(1024)S(1)} %add_rsqrt_fusion), kind=kOutput, calls=%fused_computation.29 | convolution fusion | flops 51552190464 | bytes 90193920 | tf_op jit(solution)/shard_map/while/body/eval_jaxpr/cond/branch_1_fun/dot_general | solution.py:77
  789.5 62.0 %multiply_convert_fusion.clone.6 = bf16[1024,8192]{1,0:T(8,128)(2,1)} fusion(f32[1024,8192]{1,0:T(8,128)} %fusion.23, bf16[1,3072,8192]{2,1,0:T(8,128)(2,1)} %get-tuple-element.450, bf16[1024,3072]{1,0:T(8,128)(2,1)S(1)} %copy-done.3, f32[3072]{0:T(1024)S(1)} %bitcast.124, f32[1024]{0:T(1024)S(1)} %add_rsqrt_fusion), kind=kOutput, calls=%fused_computation.31.clone.clone.clone.clone.clone.1 | convolution fusion | flops 51602522112 | bytes 106971136 | tf_op jit(solution)/shard_map/while/body/eval_jaxpr/cond/branch_1_fun/dot_general | solution.py:78
  851.5 62.1 %fusion.38 = bf16[1024,3072]{1,0:T(8,128)(2,1)} fusion(bf16[1024,3072]{1,0:T(8,128)(2,1)S(1)} %copy-done.3, bf16[1,8192,3072]{2,1,0:T(8,128)(2,1)} %get-tuple-element.451, bf16[1024,8192]{1,0:T(8,128)(2,1)} %multiply_convert_fusion.clone.6), kind=kOutput, calls=%fused_computation.47 | convolution fusion | flops 51549044736 | bytes 79691776 | tf_op jit(solution)/shard_map/while/body/eval_jaxpr/cond/branch_1_fun/dot_general | solution.py:80
  915.9 121.9 %collective-permute-done = bf16[1024,3072]{1,0:T(8,128)(2,1)} collective-permute-done((bf16[1024,3072]{1,0:T(8,128)(2,1)}, bf16[1024,3072]{1,0:T(8,128)(2,1)}, u32[]{:S(2)}, u32[]{:S(2)}) %collective-permute-start) | collective-permute-done | bytes 6291488 | tf_op jit(solution)/shard_map/while/body/eval_jaxpr/ppermute | solution.py:134
  1048.2 525.8 %conditional.4 = ((bf16[1024,3072]{1,0:T(8,128)(2,1)}, bf16[1,4096,8,128]{3,1,2,0:T(8,128)(2,1)}, bf16[1,4096,8,128]{3,1,2,0:T(8,128)(2,1)})) conditional(s32[]{:T(128)} %convert_element_type.145, (bf16[1024,3072]{1,0:T(8,128)(2,1)}, bf16[1,4096,8,128]{3,1,2,0:T(8,128)(2,1)}, bf16[1,4096,8,128]{3,1,2,0:T(8,128)(2,1)}) %tuple.85, ...), branch_computations={%region_1.1_spmd, %region_2.8_spmd} | conditional | flops 219520565248 | bytes 888622080 | solution.py:130
  1129.3 229.9 %while.37 = (s32[]{:T(128)}, f32[8,3,1024]{2,1,0:T(4,128)S(1)}, f32[8,3,1024]{2,1,0:T(4,128)S(1)}, f32[8,3,1024,128]{3,2,1,0:T(8,128)}, s32[]{:T(128)}, /*index=...) while((s32[]{:T(128)}, f32[8,3,1024]{2,1,0:T(4,128)S(1)}, ...), condition=%wide.region_7.6_spmd.clone, body=%wide.region_4.5_spmd.clone.sunk | while | flops 13170167808 | bytes 343427264 | solution.py:69
  1314.4 44.6 multiply_add_fusion.5
  1389.4 60.3 %fusion.23 = f32[1024,8192]{1,0:T(8,128)} fusion(bf16[1,3072,8192]{2,1,0:T(8,128)(2,1)} %get-tuple-element.449, bf16[1024,3072]{1,0:T(8,128)(2,1)} %get-tuple-element.614, f32[3072]{0:T(1024)S(1)} %bitcast.123, f32[1024]{0:T(1024)S(1)} %add_rsqrt_fusion), kind=kOutput, calls=%fused_computation.29 | convolution fusion | flops 51552190464 | bytes 90193920 | tf_op jit(solution)/shard_map/while/body/eval_jaxpr/cond/branch_1_fun/dot_general | solution.py:77
  1449.7 62.0 %multiply_convert_fusion.clone.6 = bf16[1024,8192]{1,0:T(8,128)(2,1)} fusion(f32[1024,8192]{1,0:T(8,128)} %fusion.23, bf16[1,3072,8192]{2,1,0:T(8,128)(2,1)} %get-tuple-element.450, bf16[1024,3072]{1,0:T(8,128)(2,1)S(1)} %copy-done.3, f32[3072]{0:T(1024)S(1)} %bitcast.124, f32[1024]{0:T(1024)S(1)} %add_rsqrt_fusion), kind=kOutput, calls=%fused_computation.31.clone.clone.clone.clone.clone.1 | convolution fusion | flops 51602522112 | bytes 106971136 | tf_op jit(solution)/shard_map/while/body/eval_jaxpr/cond/branch_1_fun/dot_general | solution.py:78
  1511.7 62.1 %fusion.38 = bf16[1024,3072]{1,0:T(8,128)(2,1)} fusion(bf16[1024,3072]{1,0:T(8,128)(2,1)S(1)} %copy-done.3, bf16[1,8192,3072]{2,1,0:T(8,128)(2,1)} %get-tuple-element.451, bf16[1024,8192]{1,0:T(8,128)(2,1)} %multiply_convert_fusion.clone.6), kind=kOutput, calls=%fused_computation.47 | convolution fusion | flops 51549044736 | bytes 79691776 | tf_op jit(solution)/shard_map/while/body/eval_jaxpr/cond/branch_1_fun/dot_general | solution.py:80
  1575.9 122.4 %collective-permute-done = bf16[1024,3072]{1,0:T(8,128)(2,1)} collective-permute-done((bf16[1024,3072]{1,0:T(8,128)(2,1)}, bf16[1024,3072]{1,0:T(8,128)(2,1)}, u32[]{:S(2)}, u32[]{:S(2)}) %collective-permute-start) | collective-permute-done | bytes 6291488 | tf_op jit(solution)/shard_map/while/body/eval_jaxpr/ppermute | solution.py:134
  1708.9 640.6 %conditional.4 = ((bf16[1024,3072]{1,0:T(8,128)(2,1)}, bf16[1,4096,8,128]{3,1,2,0:T(8,128)(2,1)}, bf16[1,4096,8,128]{3,1,2,0:T(8,128)(2,1)})) conditional(s32[]{:T(128)} %convert_element_type.145, (bf16[1024,3072]{1,0:T(8,128)(2,1)}, bf16[1,4096,8,128]{3,1,2,0:T(8,128)(2,1)}, bf16[1,4096,8,128]{3,1,2,0:T(8,128)(2,1)}) %tuple.85, ...), branch_computations={%region_1.1_spmd, %region_2.8_spmd} | conditional | flops 219520565248 | bytes 888622080 | solution.py:130
  1789.9 345.0 %while.37 = (s32[]{:T(128)}, f32[8,3,1024]{2,1,0:T(4,128)S(1)}, f32[8,3,1024]{2,1,0:T(4,128)S(1)}, f32[8,3,1024,128]{3,2,1,0:T(8,128)}, s32[]{:T(128)}, /*index=...) while((s32[]{:T(128)}, f32[8,3,1024]{2,1,0:T(4,128)S(1)}, ...), condition=%wide.region_7.6_spmd.clone, body=%wide.region_4.5_spmd.clone.sunk | while | flops 13170167808 | bytes 343427264 | solution.py:69
  2165.0 60.3 %fusion.23 = f32[1024,8192]{1,0:T(8,128)} fusion(bf16[1,3072,8192]{2,1,0:T(8,128)(2,1)} %get-tuple-element.449, bf16[1024,3072]{1,0:T(8,128)(2,1)} %get-tuple-element.614, f32[3072]{0:T(1024)S(1)} %bitcast.123, f32[1024]{0:T(1024)S(1)} %add_rsqrt_fusion), kind=kOutput, calls=%fused_computation.29 | convolution fusion | flops 51552190464 | bytes 90193920 | tf_op jit(solution)/shard_map/while/body/eval_jaxpr/cond/branch_1_fun/dot_general | solution.py:77
  2225.3 61.9 %multiply_convert_fusion.clone.6 = bf16[1024,8192]{1,0:T(8,128)(2,1)} fusion(f32[1024,8192]{1,0:T(8,128)} %fusion.23, bf16[1,3072,8192]{2,1,0:T(8,128)(2,1)} %get-tuple-element.450, bf16[1024,3072]{1,0:T(8,128)(2,1)S(1)} %copy-done.3, f32[3072]{0:T(1024)S(1)} %bitcast.124, f32[1024]{0:T(1024)S(1)} %add_rsqrt_fusion), kind=kOutput, calls=%fused_computation.31.clone.clone.clone.clone.clone.1 | convolution fusion | flops 51602522112 | bytes 106971136 | tf_op jit(solution)/shard_map/while/body/eval_jaxpr/cond/branch_1_fun/dot_general | solution.py:78
  2287.2 62.1 %fusion.38 = bf16[1024,3072]{1,0:T(8,128)(2,1)} fusion(bf16[1024,3072]{1,0:T(8,128)(2,1)S(1)} %copy-done.3, bf16[1,8192,3072]{2,1,0:T(8,128)(2,1)} %get-tuple-element.451, bf16[1024,8192]{1,0:T(8,128)(2,1)} %multiply_convert_fusion.clone.6), kind=kOutput, calls=%fused_computation.47 | convolution fusion | flops 51549044736 | bytes 79691776 | tf_op jit(solution)/shard_map/while/body/eval_jaxpr/cond/branch_1_fun/dot_general | solution.py:80
  2351.5 122.4 %collective-permute-done = bf16[1024,3072]{1,0:T(8,128)(2,1)} collective-permute-done((bf16[1024,3072]{1,0:T(8,128)(2,1)}, bf16[1024,3072]{1,0:T(8,128)(2,1)}, u32[]{:S(2)}, u32[]{:S(2)}) %collective-permute-start) | collective-permute-done | bytes 6291488 | tf_op jit(solution)/shard_map/while/body/eval_jaxpr/ppermute | solution.py:134
  2484.3 755.9 %conditional.4 = ((bf16[1024,3072]{1,0:T(8,128)(2,1)}, bf16[1,4096,8,128]{3,1,2,0:T(8,128)(2,1)}, bf16[1,4096,8,128]{3,1,2,0:T(8,128)(2,1)})) conditional(s32[]{:T(128)} %convert_element_type.145, (bf16[1024,3072]{1,0:T(8,128)(2,1)}, bf16[1,4096,8,128]{3,1,2,0:T(8,128)(2,1)}, bf16[1,4096,8,128]{3,1,2,0:T(8,128)(2,1)}) %tuple.85, ...), branch_computations={%region_1.1_spmd, %region_2.8_spmd} | conditional | flops 219520565248 | bytes 888622080 | solution.py:130
  2565.6 459.6 %while.37 = (s32[]{:T(128)}, f32[8,3,1024]{2,1,0:T(4,128)S(1)}, f32[8,3,1024]{2,1,0:T(4,128)S(1)}, f32[8,3,1024,128]{3,2,1,0:T(8,128)}, s32[]{:T(128)}, /*index=...) while((s32[]{:T(128)}, f32[8,3,1024]{2,1,0:T(4,128)S(1)}, ...), condition=%wide.region_7.6_spmd.clone, body=%wide.region_4.5_spmd.clone.sunk | while | flops 13170167808 | bytes 343427264 | solution.py:69
  3055.3 60.3 %fusion.23 = f32[1024,8192]{1,0:T(8,128)} fusion(bf16[1,3072,8192]{2,1,0:T(8,128)(2,1)} %get-tuple-element.449, bf16[1024,3072]{1,0:T(8,128)(2,1)} %get-tuple-element.614, f32[3072]{0:T(1024)S(1)} %bitcast.123, f32[1024]{0:T(1024)S(1)} %add_rsqrt_fusion), kind=kOutput, calls=%fused_computation.29 | convolution fusion | flops 51552190464 | bytes 90193920 | tf_op jit(solution)/shard_map/while/body/eval_jaxpr/cond/branch_1_fun/dot_general | solution.py:77
  3115.7 62.0 %multiply_convert_fusion.clone.6 = bf16[1024,8192]{1,0:T(8,128)(2,1)} fusion(f32[1024,8192]{1,0:T(8,128)} %fusion.23, bf16[1,3072,8192]{2,1,0:T(8,128)(2,1)} %get-tuple-element.450, bf16[1024,3072]{1,0:T(8,128)(2,1)S(1)} %copy-done.3, f32[3072]{0:T(1024)S(1)} %bitcast.124, f32[1024]{0:T(1024)S(1)} %add_rsqrt_fusion), kind=kOutput, calls=%fused_computation.31.clone.clone.clone.clone.clone.1 | convolution fusion | flops 51602522112 | bytes 106971136 | tf_op jit(solution)/shard_map/while/body/eval_jaxpr/cond/branch_1_fun/dot_general | solution.py:78
  3177.7 62.1 %fusion.38 = bf16[1024,3072]{1,0:T(8,128)(2,1)} fusion(bf16[1024,3072]{1,0:T(8,128)(2,1)S(1)} %copy-done.3, bf16[1,8192,3072]{2,1,0:T(8,128)(2,1)} %get-tuple-element.451, bf16[1024,8192]{1,0:T(8,128)(2,1)} %multiply_convert_fusion.clone.6), kind=kOutput, calls=%fused_computation.47 | convolution fusion | flops 51549044736 | bytes 79691776 | tf_op jit(solution)/shard_map/while/body/eval_jaxpr/cond/branch_1_fun/dot_general | solution.py:80
  3242.1 67.9 %collective-permute-done = bf16[1024,3072]{1,0:T(8,128)(2,1)} collective-permute-done((bf16[1024,3072]{1,0:T(8,128)(2,1)}, bf16[1024,3072]{1,0:T(8,128)(2,1)}, u32[]{:S(2)}, u32[]{:S(2)}) %collective-permute-start) | collective-permute-done | bytes 6291488 | tf_op jit(solution)/shard_map/while/body/eval_jaxpr/ppermute | solution.py:134
  3321.6 759.1 %collective-permute-start = (bf16[1024,3072]{1,0:T(8,128)(2,1)}, bf16[1024,3072]{1,0:T(8,128)(2,1)}, u32[]{:S(2)}, u32[]{:S(2)}) collective-permute-start(bf16[1024,3072]{1,0:T(8,128)(2,1)} %get-tuple-element.791), channel_id=1, source_target_pairs={{0,1},{1,2},{2,3},{4,5},{5,6},{6,7}} | collective-permute-start | bytes 18874376 | tf_op jit(solution)/shard_map/while/body/eval_jaxpr/ppermute | solution.py:134
  4080.8 67.9 %collective-permute-done = bf16[1024,3072]{1,0:T(8,128)(2,1)} collective-permute-done((bf16[1024,3072]{1,0:T(8,128)(2,1)}, bf16[1024,3072]{1,0:T(8,128)(2,1)}, u32[]{:S(2)}, u32[]{:S(2)}) %collective-permute-start) | collective-permute-done | bytes 6291488 | tf_op jit(solution)/shard_map/while/body/eval_jaxpr/ppermute | solution.py:134
  4164.7 67.9 %collective-permute-done = bf16[1024,3072]{1,0:T(8,128)(2,1)} collective-permute-done((bf16[1024,3072]{1,0:T(8,128)(2,1)}, bf16[1024,3072]{1,0:T(8,128)(2,1)}, u32[]{:S(2)}, u32[]{:S(2)}) %collective-permute-start) | collective-permute-done | bytes 6291488 | tf_op jit(solution)/shard_map/while/body/eval_jaxpr/ppermute | solution.py:134
  4239.3 637.5 %all-to-all-start = ((bf16[4,1024,3072]{2,1,0:T(8,128)(2,1)}), bf16[4,1024,3072]{2,1,0:T(8,128)(2,1)}, u32[]{:S(2)}, u32[]{:S(2)}) async-start(bf16[4,1024,3072]{2,1,0:T(8,128)(2,1)} %get-tuple-element.484), calls=%async_computation | async-start | bytes 50331648 | tf_op jit(solution)/shard_map/all_to_all | solution.py:142
  4912.8 241.5 %all-to-all-done = bf16[4,1024,3072]{2,1,0:T(8,128)(2,1)} async-done(((bf16[4,1024,3072]{2,1,0:T(8,128)(2,1)}), bf16[4,1024,3072]{2,1,0:T(8,128)(2,1)}, u32[]{:S(2)}, u32[]{:S(2)}) %all-to-all-start) | async-done | bytes 25165856 | tf_op jit(solution)/shard_map/all_to_all | solution.py:142
  (273 shorter events, 1741.1 us)
Async XLA Ops:
  72.7 419.7 %collective-permute-start = (bf16[1024,3072]{1,0:T(8,128)(2,1)}, bf16[1024,3072]{1,0:T(8,128)(2,1)}, u32[]{:S(2)}, u32[]{:S(2)}) collective-permute-start(bf16[1024,3072]{1,0:T(8,128)(2,1)} %get-tuple-element.791), channel_id=1, source_target_pairs={{0,1},{1,2},{2,3},{4,5},{5,6},{6,7}} | collective-permute-start | bytes 18874376 | tf_op jit(solution)/shard_map/while/body/eval_jaxpr/ppermute | solution.py:134
  502.6 30.0 slice-start
  502.6 30.0 slice-start.4
  506.8 25.8 slice-start.1
  506.9 25.8 slice-start.5
  699.0 30.1 copy-start.2
  729.1 60.4 %copy-start.3 = (bf16[1024,3072]{1,0:T(8,128)(2,1)S(1)}, bf16[1024,3072]{1,0:T(8,128)(2,1)}, u32[]{:S(2)}) copy-start(bf16[1024,3072]{1,0:T(8,128)(2,1)} %get-tuple-element.614) | copy-start | bytes 18874372 | tf_op jit(solution)/shard_map/while/body/eval_jaxpr/cond
  914.0 123.8 %collective-permute-start = (bf16[1024,3072]{1,0:T(8,128)(2,1)}, bf16[1024,3072]{1,0:T(8,128)(2,1)}, u32[]{:S(2)}, u32[]{:S(2)}) collective-permute-start(bf16[1024,3072]{1,0:T(8,128)(2,1)} %get-tuple-element.791), channel_id=1, source_target_pairs={{0,1},{1,2},{2,3},{4,5},{5,6},{6,7}} | collective-permute-start | bytes 18874376 | tf_op jit(solution)/shard_map/while/body/eval_jaxpr/ppermute | solution.py:134
  1048.2 29.6 slice-start
  1048.2 29.6 slice-start.4
  1052.4 25.4 slice-start.1
  1052.4 25.4 slice-start.5
  1359.2 30.1 copy-start.2
  1389.4 60.4 %copy-start.3 = (bf16[1024,3072]{1,0:T(8,128)(2,1)S(1)}, bf16[1024,3072]{1,0:T(8,128)(2,1)}, u32[]{:S(2)}) copy-start(bf16[1024,3072]{1,0:T(8,128)(2,1)} %get-tuple-element.614) | copy-start | bytes 18874372 | tf_op jit(solution)/shard_map/while/body/eval_jaxpr/cond
  1574.0 124.3 %collective-permute-start = (bf16[1024,3072]{1,0:T(8,128)(2,1)}, bf16[1024,3072]{1,0:T(8,128)(2,1)}, u32[]{:S(2)}, u32[]{:S(2)}) collective-permute-start(bf16[1024,3072]{1,0:T(8,128)(2,1)} %get-tuple-element.791), channel_id=1, source_target_pairs={{0,1},{1,2},{2,3},{4,5},{5,6},{6,7}} | collective-permute-start | bytes 18874376 | tf_op jit(solution)/shard_map/while/body/eval_jaxpr/ppermute | solution.py:134
  1708.9 29.6 slice-start
  1709.0 29.6 slice-start.4
  1713.2 25.3 slice-start.1
  1713.2 25.3 slice-start.5
  2134.9 30.1 copy-start.2
  2165.0 60.4 %copy-start.3 = (bf16[1024,3072]{1,0:T(8,128)(2,1)S(1)}, bf16[1024,3072]{1,0:T(8,128)(2,1)}, u32[]{:S(2)}) copy-start(bf16[1024,3072]{1,0:T(8,128)(2,1)} %get-tuple-element.614) | copy-start | bytes 18874372 | tf_op jit(solution)/shard_map/while/body/eval_jaxpr/cond
  2349.5 124.3 %collective-permute-start = (bf16[1024,3072]{1,0:T(8,128)(2,1)}, bf16[1024,3072]{1,0:T(8,128)(2,1)}, u32[]{:S(2)}, u32[]{:S(2)}) collective-permute-start(bf16[1024,3072]{1,0:T(8,128)(2,1)} %get-tuple-element.791), channel_id=1, source_target_pairs={{0,1},{1,2},{2,3},{4,5},{5,6},{6,7}} | collective-permute-start | bytes 18874376 | tf_op jit(solution)/shard_map/while/body/eval_jaxpr/ppermute | solution.py:134
  2484.3 29.9 slice-start
  2484.3 29.9 slice-start.4
  2488.5 25.7 slice-start.1
  2488.5 25.7 slice-start.5
  3025.2 30.1 copy-start.2
  3055.3 60.4 %copy-start.3 = (bf16[1024,3072]{1,0:T(8,128)(2,1)S(1)}, bf16[1024,3072]{1,0:T(8,128)(2,1)}, u32[]{:S(2)}) copy-start(bf16[1024,3072]{1,0:T(8,128)(2,1)} %get-tuple-element.614) | copy-start | bytes 18874372 | tf_op jit(solution)/shard_map/while/body/eval_jaxpr/cond
  3240.2 69.8 %collective-permute-start = (bf16[1024,3072]{1,0:T(8,128)(2,1)}, bf16[1024,3072]{1,0:T(8,128)(2,1)}, u32[]{:S(2)}, u32[]{:S(2)}) collective-permute-start(bf16[1024,3072]{1,0:T(8,128)(2,1)} %get-tuple-element.791), channel_id=1, source_target_pairs={{0,1},{1,2},{2,3},{4,5},{5,6},{6,7}} | collective-permute-start | bytes 18874376 | tf_op jit(solution)/shard_map/while/body/eval_jaxpr/ppermute | solution.py:134
  3321.6 827.0 %collective-permute-start = (bf16[1024,3072]{1,0:T(8,128)(2,1)}, bf16[1024,3072]{1,0:T(8,128)(2,1)}, u32[]{:S(2)}, u32[]{:S(2)}) collective-permute-start(bf16[1024,3072]{1,0:T(8,128)(2,1)} %get-tuple-element.791), channel_id=1, source_target_pairs={{0,1},{1,2},{2,3},{4,5},{5,6},{6,7}} | collective-permute-start | bytes 18874376 | tf_op jit(solution)/shard_map/while/body/eval_jaxpr/ppermute | solution.py:134
  4158.7 73.8 %collective-permute-start = (bf16[1024,3072]{1,0:T(8,128)(2,1)}, bf16[1024,3072]{1,0:T(8,128)(2,1)}, u32[]{:S(2)}, u32[]{:S(2)}) collective-permute-start(bf16[1024,3072]{1,0:T(8,128)(2,1)} %get-tuple-element.791), channel_id=1, source_target_pairs={{0,1},{1,2},{2,3},{4,5},{5,6},{6,7}} | collective-permute-start | bytes 18874376 | tf_op jit(solution)/shard_map/while/body/eval_jaxpr/ppermute | solution.py:134
  4239.3 915.0 %all-to-all-start = ((bf16[4,1024,3072]{2,1,0:T(8,128)(2,1)}), bf16[4,1024,3072]{2,1,0:T(8,128)(2,1)}, u32[]{:S(2)}, u32[]{:S(2)}) async-start(bf16[4,1024,3072]{2,1,0:T(8,128)(2,1)} %get-tuple-element.484), calls=%async_computation | async-start | bytes 50331648 | tf_op jit(solution)/shard_map/all_to_all | solution.py:142
  (7 other events, 78.0 us)
where the time goes:
time: 5170 us; the launch traced here: 5160 us
  matrix products  1850 us (36%)
  starting transfers between devices  1410 us (27%)
  waiting for transfers between devices  1230 us (24%)
  other arithmetic  468 us (9%)
  local copies, waits for them, and re-layouts  183 us (4%)
    ppermute x7, waiting for transfers between devices, tick_fn(): recv_buf = lax.ppermute(hidden_out, 'stage', send_pairs)  986 us
    ppermute x7, starting transfers between devices, tick_fn(): recv_buf = lax.ppermute(hidden_out, 'stage', send_pairs)  776 us
    all_to_all x1, starting transfers between devices, stage_program(): delivered = lax.all_to_all(out_blocks, 'stage', 0, 0, tiled=True)  638 us
    dot_general x10, matrix products, key_step(): jnp.einsum('hgqk,khd->hgqd', probs_blk.astype(jnp.bfloat16), value_blk, p...  446 us
    dot_general x10, matrix products, key_step(): jnp.einsum('qhgd,khd->hgqk', q_block, key_blk, preferred_element_type=jnp...  371 us
    reduce_sum x10, other arithmetic, key_step(): run_sum = run_sum * rescale + jnp.sum(probs_blk, axis=-1)  313 us
    dot_general x4, matrix products, mlp_block(): jnp.dot(act_val, w_down[layer_idx], preferred_element_type=jnp.float32)  248 us
    dot_general x4, matrix products, mlp_block(): jnp.dot(normed, w_up[layer_idx], preferred_element_type=jnp.float32)  248 us
  transfers between devices with their start and end apart: 8, of which 8 were waited for; matrix products, arithmetic and copies ran while one was open for 1% of the time, Pallas kernels for 0%

commit v1 on v0

v1 whole, which is shorter than its diff:
```python
import functools
import jax
import jax.numpy as jnp
from jax import lax
from jax.experimental import pallas as pl
from jax.experimental.pallas import tpu as pltpu
from jax.sharding import PartitionSpec as P

EPS = 1e-5
ROPE_BASE = 10000.0
NEG_BIG = -1e30
LOG2E = 1.4426950408889634
BLK = 256
KB = 512
WC = 512
DC = 256
NS = 6
NG = 3
ND = 4


def normed(hidden, gain):
    hid32 = hidden.astype(jnp.float32)
    inv_rms = lax.rsqrt(jnp.mean(hid32 * hid32, axis=-1, keepdims=True) + EPS)
    return (hid32 * inv_rms * gain).astype(jnp.bfloat16)


def dot(a, b):
    return jnp.dot(a, b, preferred_element_type=jnp.float32)


def alloc_kernel(*refs):
    pass


def attn_kernel(tick, base, emb, recv, gain, cos_hbm, sin_hbm, wq, wk, wv, wo, fin, hlast, kt_in, vw_in, kc_in, vc_in, out_in,
                h1, staged, kt, vw, kc, vc, out,
                hin, a, qs, knt, vn, kvf, kst, vst, ob, relay, wbuf, ktbuf, vbuf, cosb, sinb, s_a, s_b, m_a, m_b, l_s, acc_s,
                wsem, ksem, vsem, hsem, csem, osem, fsem):
    valid, stage = base[0], base[1]
    stages = base[2]
    d_model = wq.shape[0]
    kv_heads, head_dim, seq_len = kt.shape
    group = wq.shape[1] // (kv_heads * head_dim)
    rows3 = group * BLK
    n_blocks = seq_len // BLK
    per_owner = out.shape[0] // BLK
    per = WC // head_dim
    n_q, n_k, n_o = wq.shape[1] // WC, wk.shape[1] // WC, wo.shape[1] // WC
    max_kb = s_a.shape[0]
    bounds = [(0, wq), (n_q, wk), (n_q + n_k, wv), (n_q + 2 * n_k, wo)]
    total = n_q + 2 * n_k + n_o
    ends = [b[0] for b in bounds[1:]] + [total]
    scale2 = head_dim ** -0.5 * LOG2E
    blk_raw = tick[0] - stage
    blk = jnp.clip(blk_raw, 0, n_blocks - 1)
    active = (blk_raw >= 0) & (blk_raw < n_blocks)
    is_last = stage == stages - 1

    def wcopy(ref, col, slot):
        return pltpu.make_async_copy(ref.at[:, pl.ds(pl.multiple_of(col * WC, WC), WC)], wbuf.at[slot], wsem.at[slot])

    def wstart(c):
        for (lo, ref), hi in zip(bounds, ends):
            if isinstance(c, int):
                if lo <= c < hi:
                    wcopy(ref, c - lo, c % NS).start()
            else:
                @pl.when((c >= lo) & (c < hi))
                def _():
                    wcopy(ref, c - lo, lax.rem(c, NS)).start()

    def wwait(c):
        wcopy(wq, 0, lax.rem(c, NS)).wait()

    pos = pl.multiple_of(blk * BLK, BLK)
    nkb = jnp.minimum(jnp.minimum((pos + BLK + KB - 1) // KB, (valid + KB - 1) // KB), max_kb)
    nfull = jnp.minimum((pos + 1) // KB, valid // KB)

    def emb_copy():
        return pltpu.make_async_copy(emb.at[pl.ds(pos, BLK), :], hin, hsem.at[0])

    def recv_copy(i):
        return pltpu.make_async_copy(recv.at[i], hin.at[:, pl.ds(i * DC, DC)], hsem.at[i])

    @pl.when(active & (stage == 0))
    def _():
        emb_copy().start()

    @pl.when(active & (stage != 0))
    def _():
        for i in range(d_model // DC):
            recv_copy(i).start()

    ccopy = pltpu.make_async_copy(cos_hbm.at[pl.ds(pos, BLK), :], cosb, csem.at[0])
    scopy = pltpu.make_async_copy(sin_hbm.at[pl.ds(pos, BLK), :], sinb, csem.at[1])

    def kt_copy(h, slot, kb):
        return pltpu.make_async_copy(kt.at[h, :, pl.ds(pl.multiple_of(kb * KB, KB), KB)], ktbuf.at[slot, kb], ksem.at[slot, kb])

    def v_copy(h, slot, kb):
        rows = pl.ds(pl.multiple_of(kb * KB, KB), KB)
        return pltpu.make_async_copy(vw.at[h, rows, :], vbuf.at[slot, rows, :], vsem.at[slot, kb])

    def over_kb(make, h, slot, act):
        def body(kb, carry):
            getattr(make(h, slot, kb), act)()
            return carry
        lax.fori_loop(0, nkb, body, 0)

    @pl.when(active)
    def _():
        ccopy.start()
        scopy.start()
        for c in range(NS):
            wstart(c)
        over_kb(kt_copy, 0, 0, 'start')
        over_kb(v_copy, 0, 0, 'start')
        over_kb(kt_copy, 1, 1, 'start')

    done_blk = jnp.where(is_last, tick[0] - stages, tick[0] - stages - 1)
    own_row = done_blk - stage * per_owner
    mine = (own_row >= 0) & (own_row < per_owner)
    own_row = pl.multiple_of(jnp.clip(own_row, 0, per_owner - 1) * BLK, BLK)
    relay_in = pltpu.make_async_copy(hlast, relay, fsem.at[0])
    relay_fin = pltpu.make_async_copy(fin, relay, fsem.at[0])
    relay_stage = pltpu.make_async_copy(relay, staged, fsem.at[1])
    relay_out = pltpu.make_async_copy(relay, out.at[pl.ds(own_row, BLK), :], fsem.at[2])

    mine = mine & active
    last_active = is_last & active
    fin_active = mine & jnp.logical_not(is_last)

    @pl.when(last_active)
    def _():
        relay_in.start()

    @pl.when(fin_active)
    def _():
        relay_fin.start()

    @pl.when(active & (stage == 0))
    def _():
        emb_copy().wait()

    @pl.when(active & (stage != 0))
    def _():
        for i in range(d_model // DC):
            recv_copy(i).wait()

    @pl.when(active)
    def _():
        a[...] = normed(hin[...], gain[...])
        ccopy.wait()
        scopy.wait()

        def rope(x):
            return x * cosb[...] + pltpu.roll(x, head_dim // 2, 1) * sinb[...]

        def pair_of(lhs, j, use):
            c = 2 * j
            wwait(c)
            wwait(c + 1)
            accs = [dot(lhs[...], wbuf[lax.rem(c + i, NS)]) for i in range(2)]
            for i in range(2):
                use(c + i, accs[i])

        def q_use(c, acc):
            for i in range(per):
                qs[c * per + i] = rope(acc[:, i * head_dim:(i + 1) * head_dim]).astype(jnp.bfloat16)

        def k_use(c, acc):
            for i in range(per):
                h = (c - n_q) * per + i
                x = rope(acc[:, i * head_dim:(i + 1) * head_dim])
                kvf[pl.ds(h, BLK, stride=kv_heads), :] = x
                knt[h] = x.T.astype(jnp.bfloat16)

        def v_use(c, acc):
            for i in range(per):
                h = (c - n_q - n_k) * per + i
                x = acc[:, i * head_dim:(i + 1) * head_dim]
                kvf[pl.ds(h, BLK, stride=kv_heads), :] = x
                vn[h] = x.astype(jnp.bfloat16)

        def project(use):
            def body(j, carry):
                pair_of(a, j, use)
                wstart(2 * j + NS)
                wstart(2 * j + 1 + NS)
                return carry
            return body

        q_step, k_step, v_step = project(q_use), project(k_use), project(v_use)

        cache_rows = pl.ds(pl.multiple_of(pos * kv_heads, BLK), BLK * kv_heads)
        k_out = pltpu.make_async_copy(kst, kc.at[cache_rows, :], osem.at[0])
        v_out = pltpu.make_async_copy(vst, vc.at[cache_rows, :], osem.at[1])
        kt_out = pltpu.make_async_copy(knt, kt.at[:, :, pl.ds(pos, BLK)], osem.at[2])
        vw_out = pltpu.make_async_copy(vn, vw.at[:, pl.ds(pos, BLK), :], osem.at[3])

        lax.fori_loop(0, n_q // 2, q_step, 0)
        lax.fori_loop(n_q // 2, (n_q + n_k) // 2, k_step, 0)
        kst[...] = kvf[...].astype(jnp.bfloat16)
        k_out.start()
        lax.fori_loop((n_q + n_k) // 2, (n_q + 2 * n_k) // 2, v_step, 0)
        vst[...] = kvf[...].astype(jnp.bfloat16)
        v_out.start()

        @pl.when(last_active)
        def _():
            relay_in.wait()
            relay_stage.start()

        @pl.when(fin_active)
        def _():
            relay_fin.wait()

        @pl.when(mine)
        def _():
            relay_out.start()

        has_self = pos < nkb * KB
        self_kb = pos // KB
        self_off = pl.multiple_of(pos - self_kb * KB, BLK)

        def patch_k(h, slot):
            over_kb(kt_copy, h, slot, 'wait')

            @pl.when(has_self)
            def _():
                ktbuf[slot, self_kb, :, pl.ds(self_off, BLK)] = knt[h]

        def patch_v(h, slot):
            over_kb(v_copy, h, slot, 'wait')

            @pl.when(has_self)
            def _():
                vbuf[slot, pl.ds(pos, BLK), :] = vn[h]

            @pl.when(has_self & (self_off == 0))
            def _():
                vbuf[slot, pl.ds(pl.multiple_of(pos + BLK, BLK), KB - BLK), :] = jnp.zeros((KB - BLK, head_dim), jnp.bfloat16)

        def qk(h, slot, kb, s_ref, m_ref, masked):
            s = dot(qs[pl.ds(h * group, group)].reshape(rows3, head_dim), ktbuf[slot, kb])
            if masked:
                q_pos = pos + (lax.broadcasted_iota(jnp.int32, (rows3, KB), 0) & (BLK - 1))
                k_pos = kb * KB + lax.broadcasted_iota(jnp.int32, (rows3, KB), 1)
                s = jnp.where((k_pos <= q_pos) & (k_pos < valid), s, NEG_BIG)
            s = s * scale2
            s_ref[kb] = s
            parts = [s[:, i:i + head_dim] for i in range(0, KB, head_dim)]
            m_ref[...] = jnp.maximum(m_ref[...], functools.reduce(jnp.maximum, parts))

        def pv(slot, kb, s_ref, m_ref):
            top = m_ref[...]
            probs = [jnp.exp2(s_ref[kb, :, i:i + head_dim] - top) for i in range(0, KB, head_dim)]
            l_s[...] += functools.reduce(jnp.add, probs)
            pb = jnp.concatenate([x.astype(jnp.bfloat16) for x in probs], axis=1)
            acc_s[...] += dot(pb, vbuf[slot, pl.ds(pl.multiple_of(kb * KB, KB), KB), :])

        def begin(m_ref):
            m_ref[...] = jnp.full(m_ref.shape, NEG_BIG, jnp.float32)

        def top_of(m_ref):
            m_ref[...] = jnp.broadcast_to(jnp.max(m_ref[...], axis=-1, keepdims=True), m_ref.shape)
            l_s[...] = jnp.zeros(l_s.shape, jnp.float32)
            acc_s[...] = jnp.zeros(acc_s.shape, jnp.float32)

        def finish(h):
            o = acc_s[...] / jnp.sum(l_s[...], axis=-1, keepdims=True)
            for g in range(group):
                cols = pl.ds(pl.multiple_of((h * group + g) * head_dim, head_dim), head_dim)
                ob[:, cols] = o[g * BLK:(g + 1) * BLK].astype(jnp.bfloat16)

        def loops(full, edge):
            def full_body(kb, carry):
                full(kb)
                return carry

            def edge_body(kb, carry):
                edge(kb)
                return carry
            def two_body(i, carry):
                full(2 * i)
                full(2 * i + 1)
                return carry
            lax.fori_loop(0, nfull // 2, two_body, 0)
            lax.fori_loop(nfull - lax.rem(nfull, 2), nfull, full_body, 0)
            lax.fori_loop(nfull, nkb, edge_body, 0)

        def both(h, parity, prefetch):
            s_now, m_now, s_next, m_next = (s_a, m_a, s_b, m_b) if parity == 0 else (s_b, m_b, s_a, m_a)
            if prefetch:
                over_kb(kt_copy, h + 2, parity, 'start')
            over_kb(v_copy, h + 1, 1 - parity, 'start')
            patch_k(h + 1, 1 - parity)
            patch_v(h, parity)
            top_of(m_now)
            begin(m_next)

            def run(kb, masked):
                qk(h + 1, 1 - parity, kb, s_next, m_next, masked)
                pv(parity, kb, s_now, m_now)
            loops(lambda kb: run(kb, False), lambda kb: run(kb, True))
            finish(h)

        patch_k(0, 0)
        begin(m_a)
        loops(lambda kb: qk(0, 0, kb, s_a, m_a, False), lambda kb: qk(0, 0, kb, s_a, m_a, True))

        def pair(i, carry):
            both(2 * i, 0, True)
            both(2 * i + 1, 1, True)
            return carry

        lax.fori_loop(0, kv_heads // 2 - 1, pair, 0)
        both(kv_heads - 2, 0, False)
        patch_v(kv_heads - 1, 1)
        top_of(m_b)
        lax.fori_loop(0, nkb, lambda kb, carry: (pv(1, kb, s_b, m_b), carry)[1], 0)
        finish(kv_heads - 1)
        kt_out.start()
        vw_out.start()

        def o_use(c, acc):
            cols = pl.ds(pl.multiple_of((c - (total - n_o)) * WC, WC), WC)
            h1[:, cols] = (hin[:, cols].astype(jnp.float32) + acc).astype(jnp.bfloat16)

        lax.fori_loop((total - n_o) // 2, total // 2, lambda j, carry: (pair_of(ob, j, o_use), carry)[1], 0)
        k_out.wait()
        v_out.wait()
        kt_out.wait()
        vw_out.wait()

    @pl.when(last_active)
    def _():
        relay_stage.wait()

    @pl.when(mine)
    def _():
        relay_out.wait()


def mlp_kernel(stages, h1, gain, staged, wg, wu, wd, hout, recv, fin, b, act, hbuf, gbuf, ubuf, dbuf, gsem, usem, dsem, ssem, rsem, fssem, frsem):
    stage = lax.axis_index('stage')
    d_ff = wg.shape[1]
    n_g, n_d = d_ff // WC, wd.shape[1] // DC
    barrier = pltpu.get_barrier_semaphore()

    @pl.when(stage > 0)
    def _():
        pl.semaphore_signal(barrier, inc=1, device_id={'stage': stage - 1}, device_id_type=pl.DeviceIdType.MESH)

    @pl.when(stage < stages - 1)
    def _():
        pl.semaphore_signal(barrier, inc=1, device_id={'stage': stages - 1}, device_id_type=pl.DeviceIdType.MESH)

    def deliver(i):
        return pltpu.make_async_remote_copy(src_ref=staged, dst_ref=fin, send_sem=fssem.at[i], recv_sem=frsem.at[0],
                                            device_id={'stage': i}, device_id_type=pl.DeviceIdType.MESH)

    def gu_copies(c, slot):
        cols = pl.ds(pl.multiple_of(c * WC, WC), WC)
        return (pltpu.make_async_copy(wg.at[:, cols], gbuf.at[slot], gsem.at[slot]),
                pltpu.make_async_copy(wu.at[:, cols], ubuf.at[slot], usem.at[slot]))

    def d_copy(c, slot):
        return pltpu.make_async_copy(wd.at[:, pl.ds(pl.multiple_of(c * DC, DC), DC)], dbuf.at[slot], dsem.at[slot])

    for c in range(NG):
        for cp in gu_copies(c, c):
            cp.start()
    b[...] = normed(h1[...], gain[...])

    def gate_up(c, carry):
        slot = lax.rem(c, NG)

        @pl.when((c == 1) & (stage < stages - 1))
        def _():
            pl.semaphore_wait(barrier, 1)

        @pl.when((c == 1) & (stage == stages - 1))
        def _():
            pl.semaphore_wait(barrier, stages - 1)
            for i in range(stages - 1):
                deliver(i).start()

        for cp in gu_copies(c, slot):
            cp.wait()
        gate = dot(b[...], gbuf[slot])
        up = dot(b[...], ubuf[slot])
        act[:, pl.ds(pl.multiple_of(c * WC, WC), WC)] = (jax.nn.silu(gate) * up).astype(jnp.bfloat16)

        @pl.when(c + NG < n_g)
        def _():
            for cp in gu_copies(c + NG, slot):
                cp.start()

        @pl.when(c >= n_g - ND)
        def _():
            d_copy(c - (n_g - ND), c - (n_g - ND)).start()
        return carry

    lax.fori_loop(0, n_g, gate_up, 0)

    def send(c):
        return pltpu.make_async_remote_copy(src_ref=hbuf.at[c], dst_ref=recv.at[c], send_sem=ssem.at[c], recv_sem=rsem.at[c],
                                            device_id={'stage': lax.rem(stage + 1, stages)}, device_id_type=pl.DeviceIdType.MESH)

    def down(c, carry):
        slot = lax.rem(c, ND)
        d_copy(c, slot).wait()
        cols = pl.ds(pl.multiple_of(c * DC, DC), DC)
        y = (h1[:, cols].astype(jnp.float32) + dot(act[...], dbuf[slot])).astype(jnp.bfloat16)
        hbuf[c] = y
        hout[:, cols] = y

        @pl.when(c + ND < n_d)
        def _():
            d_copy(c + ND, slot).start()

        @pl.when(stage < stages - 1)
        def _():
            send(c).start()
        return carry

    lax.fori_loop(0, n_d, down, 0)

    @pl.when(stage < stages - 1)
    def _():
        for c in range(n_d):
            send(c).wait_send()
        deliver(0).wait_recv()

    @pl.when(stage == stages - 1)
    def _():
        for i in range(stages - 1):
            deliver(i).wait_send()

    @pl.when(stage > 0)
    def _():
        for c in range(n_d):
            send(c).wait_recv()


def solution(mesh):
    stages = mesh.shape['stage']
    gain_spec = P('stage', None)
    spec_three = P('stage', None, None)
    spec_four = P('stage', None, None, None)
    any_spec = pl.BlockSpec(memory_space=pl.ANY)
    vmem_spec = pl.BlockSpec(memory_space=pltpu.VMEM)
    smem_spec = pl.BlockSpec(memory_space=pltpu.SMEM)
    bf16, f32 = jnp.bfloat16, jnp.float32

    def stage_program(embeddings, valid_len, attn_gain, w_q, w_k, w_v, w_o, mlp_gain, w_gate, w_up, w_down):
        seq_len, d_model = embeddings.shape
        kv_heads, head_dim = w_k.shape[2], w_k.shape[3]
        heads = w_q.shape[2]
        group = heads // kv_heads
        d_ff = w_gate.shape[2]
        n_blocks = seq_len // BLK
        per_owner = n_blocks // stages
        n_d = d_model // DC
        stage = lax.axis_index('stage')

        wq = w_q[0].reshape(d_model, heads * head_dim)
        wk = w_k[0].reshape(d_model, kv_heads * head_dim)
        wv = w_v[0].reshape(d_model, kv_heads * head_dim)
        wo = w_o[0].reshape(heads * head_dim, d_model)
        wg, wu, wd = w_gate[0], w_up[0], w_down[0]

        half = head_dim // 2
        inv_freq = ROPE_BASE ** (-jnp.arange(half, dtype=f32) * (2.0 / head_dim))
        angles = jnp.arange(seq_len).astype(f32)[:, None] * inv_freq[None, :]
        cos_tab, sin_tab = jnp.cos(angles), jnp.sin(angles)
        cos_full = jnp.concatenate([cos_tab, cos_tab], axis=1)
        sin_full = jnp.concatenate([-sin_tab, sin_tab], axis=1)

        max_kb = -(-(seq_len - seq_len // 8) // KB)
        rows3 = group * BLK
        hid = jax.ShapeDtypeStruct((BLK, d_model), bf16)
        chunks = jax.ShapeDtypeStruct((n_d, BLK, DC), bf16)
        kt_t = jax.ShapeDtypeStruct((kv_heads, head_dim, seq_len), bf16)
        vw_t = jax.ShapeDtypeStruct((kv_heads, seq_len, head_dim), bf16)
        cache_t = jax.ShapeDtypeStruct((seq_len * kv_heads, head_dim), bf16)
        out_t = jax.ShapeDtypeStruct((per_owner * BLK, d_model), bf16)

        def vmem(*shape, dtype=bf16):
            return pltpu.VMEM(shape, dtype)

        def dma(*shape):
            return pltpu.SemaphoreType.DMA(shape)

        attn_call = pl.pallas_call(
            attn_kernel,
            out_shape=(hid, hid, kt_t, vw_t, cache_t, cache_t, out_t),
            in_specs=[smem_spec, smem_spec, any_spec, any_spec, vmem_spec] + [any_spec] * 13,
            out_specs=(vmem_spec,) + (any_spec,) * 6,
            input_output_aliases={13: 2, 14: 3, 15: 4, 16: 5, 17: 6},
            scratch_shapes=[
                vmem(BLK, d_model), vmem(BLK, d_model), vmem(heads, BLK, head_dim),
                vmem(kv_heads, head_dim, BLK), vmem(kv_heads, BLK, head_dim),
                vmem(BLK * kv_heads, head_dim, dtype=f32), vmem(BLK * kv_heads, head_dim), vmem(BLK * kv_heads, head_dim),
                vmem(BLK, d_model), vmem(BLK, d_model),
                vmem(NS, d_model, WC),
                vmem(2, max_kb, head_dim, KB), vmem(2, max_kb * KB, head_dim),
                vmem(BLK, head_dim, dtype=f32), vmem(BLK, head_dim, dtype=f32),
                vmem(max_kb, rows3, KB, dtype=f32), vmem(max_kb, rows3, KB, dtype=f32),
                vmem(rows3, head_dim, dtype=f32), vmem(rows3, head_dim, dtype=f32),
                vmem(rows3, head_dim, dtype=f32), vmem(rows3, head_dim, dtype=f32),
                dma(NS), dma(2, max_kb), dma(2, max_kb), dma(n_d), dma(2), dma(4), dma(3),
            ],
            compiler_params=pltpu.CompilerParams(vmem_limit_bytes=62 * 1024 * 1024),
            cost_estimate=pl.CostEstimate(flops=2 * BLK * d_model * (2 * d_model + 2 * kv_heads * head_dim),
                                          bytes_accessed=60 * 1024 * 1024, transcendentals=0),
            name='attn_block',
        )
        mlp_call = pl.pallas_call(
            functools.partial(mlp_kernel, stages),
            out_shape=(hid, chunks, hid),
            in_specs=[vmem_spec, vmem_spec, any_spec, any_spec, any_spec, any_spec],
            out_specs=(vmem_spec, any_spec, any_spec),
            scratch_shapes=[
                vmem(BLK, d_model), vmem(BLK, d_ff), vmem(n_d, BLK, DC),
                vmem(NG, d_model, WC), vmem(NG, d_model, WC), vmem(ND, d_ff, DC),
                dma(NG), dma(NG), dma(ND), dma(n_d), dma(n_d), dma(stages - 1), dma(1),
            ],
            compiler_params=pltpu.CompilerParams(vmem_limit_bytes=60 * 1024 * 1024, collective_id=0, has_side_effects=True),
            cost_estimate=pl.CostEstimate(flops=6 * BLK * d_model * d_ff, bytes_accessed=160 * 1024 * 1024, transcendentals=0),
            name='mlp_block',
        )
        init = pl.pallas_call(alloc_kernel, out_shape=(chunks, hid, hid, kt_t, vw_t, cache_t, cache_t, out_t),
                              out_specs=(any_spec,) * 8, name='buffers')()
        base = jnp.stack([valid_len[0], stage, jnp.int32(stages)]).astype(jnp.int32)

        def tick(tick_idx, state):
            recv, fin, hlast, kt, vw, kc, vc, out = state
            h1, staged, kt, vw, kc, vc, out = attn_call(tick_idx.reshape(1), base, embeddings, recv, attn_gain, cos_full, sin_full,
                                                        wq, wk, wv, wo, fin, hlast, kt, vw, kc, vc, out)
            hlast, recv, fin = mlp_call(h1, mlp_gain, staged, wg, wu, wd)
            return recv, fin, hlast, kt, vw, kc, vc, out

        recv, fin, hlast, kt, vw, kc, vc, out = lax.fori_loop(0, n_blocks + stages - 1, tick, tuple(init))
        row = (per_owner - 1) * BLK
        out = lax.dynamic_update_slice(out, jnp.where(stage == stages - 1, hlast, out[row:]), (row, 0))
        cache_shape = (1, seq_len, kv_heads, head_dim)
        return out, kc.reshape(cache_shape), vc.reshape(cache_shape)

    return jax.shard_map(stage_program, mesh=mesh,
                         in_specs=(P('replica', None), P('replica'), gain_spec, spec_four, spec_four, spec_four, spec_four,
                                   gain_spec, spec_three, spec_three, spec_three),
                         out_specs=(P(('replica', 'stage'), None), P('stage', 'replica', None, None), P('stage', 'replica', None, None)),
                         check_vma=False)
```

time: 5170 us -> 1940 us (0.38)
  the two profiles are of different devices: /device:TPU:5 before, /device:TPU:3 now
where the time goes in v1:
time: 1940 us
  Pallas kernels  1900 us (98%)
  local copies, waits for them, and re-layouts  24 us (1%)
    pallas_call x19, Pallas kernels, tick(): hlast, recv, fin = mlp_call(h1, mlp_gain, staged, wg, wu, wd)  1130 us
    pallas_call x19, Pallas kernels, tick(): attn_call(tick_idx.reshape(1), base, embeddings, recv, attn_gain, cos_ful...  769 us

profile of v1, /device:TPU:3, one launch (start us, length us, event | category | flops | bytes accessed | tf_op | source)
XLA Modules:
  0.0 1936.8 jit_solution(15620660578651883007)
XLA Ops:
  36.1 1897.5 %while.27 = (s32[]{:T(128)}, bf16[12,256,256]{2,1,0:T(8,128)(2,1)}, bf16[256,3072]{1,0:T(8,128)(2,1)}, bf16[256,3072]{1,0:T(8,128)(2,1)S(1)}, bf16[8,128,4096]{2...) while((s32[]{:T(128)}, bf16[12,256,256]{2,1,0:T(8,128)(2,1)}, ...), condition=%wide.region_1.0_spmd, body=%wide.region_0.0_spmd.sunk | while | flops 51539607552 | bytes 230686928 | solution.py:546
  38.7 74.7 %mlp_block.5 = (bf16[256,3072]{1,0:T(8,128)(2,1)S(1)}, bf16[12,256,256]{2,1,0:T(8,128)(2,1)}, bf16[256,3072]{1,0:T(8,128)(2,1)}) custom-call(bf16[256,3072]{1,0:T(8,128)(2,1)} %get-tuple-element.545.h1, f32[1,3072]{1,0:T(1,128)S(1)} %get-tuple-element.619.gain, bf16[256,3072]{1,0:T(8,128)(2,1)} %get-tuple-element.546.staged, ...), custom_call_target="tpu_custom_call" | custom-call | flops 38654705664 | bytes 167772160 | tf_op jit(solution)/shard_map/while/body/eval_jaxpr/mlp_block/pallas_call | solution.py:543
  115.7 81.9 %mlp_block.5 = (bf16[256,3072]{1,0:T(8,128)(2,1)S(1)}, bf16[12,256,256]{2,1,0:T(8,128)(2,1)}, bf16[256,3072]{1,0:T(8,128)(2,1)}) custom-call(bf16[256,3072]{1,0:T(8,128)(2,1)} %get-tuple-element.545.h1, f32[1,3072]{1,0:T(1,128)S(1)} %get-tuple-element.619.gain, bf16[256,3072]{1,0:T(8,128)(2,1)} %get-tuple-element.546.staged, ...), custom_call_target="tpu_custom_call" | custom-call | flops 38654705664 | bytes 167772160 | tf_op jit(solution)/shard_map/while/body/eval_jaxpr/mlp_block/pallas_call | solution.py:543
  200.0 91.8 %mlp_block.5 = (bf16[256,3072]{1,0:T(8,128)(2,1)S(1)}, bf16[12,256,256]{2,1,0:T(8,128)(2,1)}, bf16[256,3072]{1,0:T(8,128)(2,1)}) custom-call(bf16[256,3072]{1,0:T(8,128)(2,1)} %get-tuple-element.545.h1, f32[1,3072]{1,0:T(1,128)S(1)} %get-tuple-element.619.gain, bf16[256,3072]{1,0:T(8,128)(2,1)} %get-tuple-element.546.staged, ...), custom_call_target="tpu_custom_call" | custom-call | flops 38654705664 | bytes 167772160 | tf_op jit(solution)/shard_map/while/body/eval_jaxpr/mlp_block/pallas_call | solution.py:543
  326.6 52.0 %mlp_block.5 = (bf16[256,3072]{1,0:T(8,128)(2,1)S(1)}, bf16[12,256,256]{2,1,0:T(8,128)(2,1)}, bf16[256,3072]{1,0:T(8,128)(2,1)}) custom-call(bf16[256,3072]{1,0:T(8,128)(2,1)} %get-tuple-element.545.h1, f32[1,3072]{1,0:T(1,128)S(1)} %get-tuple-element.619.gain, bf16[256,3072]{1,0:T(8,128)(2,1)} %get-tuple-element.546.staged, ...), custom_call_target="tpu_custom_call" | custom-call | flops 38654705664 | bytes 167772160 | tf_op jit(solution)/shard_map/while/body/eval_jaxpr/mlp_block/pallas_call | solution.py:543
  413.4 60.5 %mlp_block.5 = (bf16[256,3072]{1,0:T(8,128)(2,1)S(1)}, bf16[12,256,256]{2,1,0:T(8,128)(2,1)}, bf16[256,3072]{1,0:T(8,128)(2,1)}) custom-call(bf16[256,3072]{1,0:T(8,128)(2,1)} %get-tuple-element.545.h1, f32[1,3072]{1,0:T(1,128)S(1)} %get-tuple-element.619.gain, bf16[256,3072]{1,0:T(8,128)(2,1)} %get-tuple-element.546.staged, ...), custom_call_target="tpu_custom_call" | custom-call | flops 38654705664 | bytes 167772160 | tf_op jit(solution)/shard_map/while/body/eval_jaxpr/mlp_block/pallas_call | solution.py:543
  512.9 52.1 %mlp_block.5 = (bf16[256,3072]{1,0:T(8,128)(2,1)S(1)}, bf16[12,256,256]{2,1,0:T(8,128)(2,1)}, bf16[256,3072]{1,0:T(8,128)(2,1)}) custom-call(bf16[256,3072]{1,0:T(8,128)(2,1)} %get-tuple-element.545.h1, f32[1,3072]{1,0:T(1,128)S(1)} %get-tuple-element.619.gain, bf16[256,3072]{1,0:T(8,128)(2,1)} %get-tuple-element.546.staged, ...), custom_call_target="tpu_custom_call" | custom-call | flops 38654705664 | bytes 167772160 | tf_op jit(solution)/shard_map/while/body/eval_jaxpr/mlp_block/pallas_call | solution.py:543
  603.9 59.4 %mlp_block.5 = (bf16[256,3072]{1,0:T(8,128)(2,1)S(1)}, bf16[12,256,256]{2,1,0:T(8,128)(2,1)}, bf16[256,3072]{1,0:T(8,128)(2,1)}) custom-call(bf16[256,3072]{1,0:T(8,128)(2,1)} %get-tuple-element.545.h1, f32[1,3072]{1,0:T(1,128)S(1)} %get-tuple-element.619.gain, bf16[256,3072]{1,0:T(8,128)(2,1)} %get-tuple-element.546.staged, ...), custom_call_target="tpu_custom_call" | custom-call | flops 38654705664 | bytes 167772160 | tf_op jit(solution)/shard_map/while/body/eval_jaxpr/mlp_block/pallas_call | solution.py:543
  663.3 42.1 %attn_block.5 = (bf16[256,3072]{1,0:T(8,128)(2,1)}, bf16[256,3072]{1,0:T(8,128)(2,1)}, bf16[8,128,4096]{2,1,0:T(8,128)(2,1)}, bf16[8,4096,128]{2,1,0:T(8,128)(2,...) custom-call(s32[1]{0:T(128)} %bitcast.22.tick, ...), custom_call_target="tpu_custom_call", output_to_operand_aliasing={{2}: (13, {}), {3}: (14, {}), {4}: (15, {}), {5}: (16, {}),... | custom-call | flops 12884901888 | bytes 62914560 | tf_op jit(solution)/shard_map/while/body/eval_jaxpr/attn_block/pallas_call | solution.py:541
  705.4 52.5 %mlp_block.5 = (bf16[256,3072]{1,0:T(8,128)(2,1)S(1)}, bf16[12,256,256]{2,1,0:T(8,128)(2,1)}, bf16[256,3072]{1,0:T(8,128)(2,1)}) custom-call(bf16[256,3072]{1,0:T(8,128)(2,1)} %get-tuple-element.545.h1, f32[1,3072]{1,0:T(1,128)S(1)} %get-tuple-element.619.gain, bf16[256,3072]{1,0:T(8,128)(2,1)} %get-tuple-element.546.staged, ...), custom_call_target="tpu_custom_call" | custom-call | flops 38654705664 | bytes 167772160 | tf_op jit(solution)/shard_map/while/body/eval_jaxpr/mlp_block/pallas_call | solution.py:543
  757.9 42.0 %attn_block.5 = (bf16[256,3072]{1,0:T(8,128)(2,1)}, bf16[256,3072]{1,0:T(8,128)(2,1)}, bf16[8,128,4096]{2,1,0:T(8,128)(2,1)}, bf16[8,4096,128]{2,1,0:T(8,128)(2,...) custom-call(s32[1]{0:T(128)} %bitcast.22.tick, ...), custom_call_target="tpu_custom_call", output_to_operand_aliasing={{2}: (13, {}), {3}: (14, {}), {4}: (15, {}), {5}: (16, {}),... | custom-call | flops 12884901888 | bytes 62914560 | tf_op jit(solution)/shard_map/while/body/eval_jaxpr/attn_block/pallas_call | solution.py:541
  799.9 62.8 %mlp_block.5 = (bf16[256,3072]{1,0:T(8,128)(2,1)S(1)}, bf16[12,256,256]{2,1,0:T(8,128)(2,1)}, bf16[256,3072]{1,0:T(8,128)(2,1)}) custom-call(bf16[256,3072]{1,0:T(8,128)(2,1)} %get-tuple-element.545.h1, f32[1,3072]{1,0:T(1,128)S(1)} %get-tuple-element.619.gain, bf16[256,3072]{1,0:T(8,128)(2,1)} %get-tuple-element.546.staged, ...), custom_call_target="tpu_custom_call" | custom-call | flops 38654705664 | bytes 167772160 | tf_op jit(solution)/shard_map/while/body/eval_jaxpr/mlp_block/pallas_call | solution.py:543
  862.8 47.1 %attn_block.5 = (bf16[256,3072]{1,0:T(8,128)(2,1)}, bf16[256,3072]{1,0:T(8,128)(2,1)}, bf16[8,128,4096]{2,1,0:T(8,128)(2,1)}, bf16[8,4096,128]{2,1,0:T(8,128)(2,...) custom-call(s32[1]{0:T(128)} %bitcast.22.tick, ...), custom_call_target="tpu_custom_call", output_to_operand_aliasing={{2}: (13, {}), {3}: (14, {}), {4}: (15, {}), {5}: (16, {}),... | custom-call | flops 12884901888 | bytes 62914560 | tf_op jit(solution)/shard_map/while/body/eval_jaxpr/attn_block/pallas_call | solution.py:541
  909.9 52.5 %mlp_block.5 = (bf16[256,3072]{1,0:T(8,128)(2,1)S(1)}, bf16[12,256,256]{2,1,0:T(8,128)(2,1)}, bf16[256,3072]{1,0:T(8,128)(2,1)}) custom-call(bf16[256,3072]{1,0:T(8,128)(2,1)} %get-tuple-element.545.h1, f32[1,3072]{1,0:T(1,128)S(1)} %get-tuple-element.619.gain, bf16[256,3072]{1,0:T(8,128)(2,1)} %get-tuple-element.546.staged, ...), custom_call_target="tpu_custom_call" | custom-call | flops 38654705664 | bytes 167772160 | tf_op jit(solution)/shard_map/while/body/eval_jaxpr/mlp_block/pallas_call | solution.py:543
  962.4 47.1 %attn_block.5 = (bf16[256,3072]{1,0:T(8,128)(2,1)}, bf16[256,3072]{1,0:T(8,128)(2,1)}, bf16[8,128,4096]{2,1,0:T(8,128)(2,1)}, bf16[8,4096,128]{2,1,0:T(8,128)(2,...) custom-call(s32[1]{0:T(128)} %bitcast.22.tick, ...), custom_call_target="tpu_custom_call", output_to_operand_aliasing={{2}: (13, {}), {3}: (14, {}), {4}: (15, {}), {5}: (16, {}),... | custom-call | flops 12884901888 | bytes 62914560 | tf_op jit(solution)/shard_map/while/body/eval_jaxpr/attn_block/pallas_call | solution.py:541
  1009.5 60.2 %mlp_block.5 = (bf16[256,3072]{1,0:T(8,128)(2,1)S(1)}, bf16[12,256,256]{2,1,0:T(8,128)(2,1)}, bf16[256,3072]{1,0:T(8,128)(2,1)}) custom-call(bf16[256,3072]{1,0:T(8,128)(2,1)} %get-tuple-element.545.h1, f32[1,3072]{1,0:T(1,128)S(1)} %get-tuple-element.619.gain, bf16[256,3072]{1,0:T(8,128)(2,1)} %get-tuple-element.546.staged, ...), custom_call_target="tpu_custom_call" | custom-call | flops 38654705664 | bytes 167772160 | tf_op jit(solution)/shard_map/while/body/eval_jaxpr/mlp_block/pallas_call | solution.py:543
  1069.7 50.9 %attn_block.5 = (bf16[256,3072]{1,0:T(8,128)(2,1)}, bf16[256,3072]{1,0:T(8,128)(2,1)}, bf16[8,128,4096]{2,1,0:T(8,128)(2,1)}, bf16[8,4096,128]{2,1,0:T(8,128)(2,...) custom-call(s32[1]{0:T(128)} %bitcast.22.tick, ...), custom_call_target="tpu_custom_call", output_to_operand_aliasing={{2}: (13, {}), {3}: (14, {}), {4}: (15, {}), {5}: (16, {}),... | custom-call | flops 12884901888 | bytes 62914560 | tf_op jit(solution)/shard_map/while/body/eval_jaxpr/attn_block/pallas_call | solution.py:541
  1120.6 52.4 %mlp_block.5 = (bf16[256,3072]{1,0:T(8,128)(2,1)S(1)}, bf16[12,256,256]{2,1,0:T(8,128)(2,1)}, bf16[256,3072]{1,0:T(8,128)(2,1)}) custom-call(bf16[256,3072]{1,0:T(8,128)(2,1)} %get-tuple-element.545.h1, f32[1,3072]{1,0:T(1,128)S(1)} %get-tuple-element.619.gain, bf16[256,3072]{1,0:T(8,128)(2,1)} %get-tuple-element.546.staged, ...), custom_call_target="tpu_custom_call" | custom-call | flops 38654705664 | bytes 167772160 | tf_op jit(solution)/shard_map/while/body/eval_jaxpr/mlp_block/pallas_call | solution.py:543
  1173.0 50.8 %attn_block.5 = (bf16[256,3072]{1,0:T(8,128)(2,1)}, bf16[256,3072]{1,0:T(8,128)(2,1)}, bf16[8,128,4096]{2,1,0:T(8,128)(2,1)}, bf16[8,4096,128]{2,1,0:T(8,128)(2,...) custom-call(s32[1]{0:T(128)} %bitcast.22.tick, ...), custom_call_target="tpu_custom_call", output_to_operand_aliasing={{2}: (13, {}), {3}: (14, {}), {4}: (15, {}), {5}: (16, {}),... | custom-call | flops 12884901888 | bytes 62914560 | tf_op jit(solution)/shard_map/while/body/eval_jaxpr/attn_block/pallas_call | solution.py:541
  1223.8 62.9 %mlp_block.5 = (bf16[256,3072]{1,0:T(8,128)(2,1)S(1)}, bf16[12,256,256]{2,1,0:T(8,128)(2,1)}, bf16[256,3072]{1,0:T(8,128)(2,1)}) custom-call(bf16[256,3072]{1,0:T(8,128)(2,1)} %get-tuple-element.545.h1, f32[1,3072]{1,0:T(1,128)S(1)} %get-tuple-element.619.gain, bf16[256,3072]{1,0:T(8,128)(2,1)} %get-tuple-element.546.staged, ...), custom_call_target="tpu_custom_call" | custom-call | flops 38654705664 | bytes 167772160 | tf_op jit(solution)/shard_map/while/body/eval_jaxpr/mlp_block/pallas_call | solution.py:543
  1286.7 55.9 %attn_block.5 = (bf16[256,3072]{1,0:T(8,128)(2,1)}, bf16[256,3072]{1,0:T(8,128)(2,1)}, bf16[8,128,4096]{2,1,0:T(8,128)(2,1)}, bf16[8,4096,128]{2,1,0:T(8,128)(2,...) custom-call(s32[1]{0:T(128)} %bitcast.22.tick, ...), custom_call_target="tpu_custom_call", output_to_operand_aliasing={{2}: (13, {}), {3}: (14, {}), {4}: (15, {}), {5}: (16, {}),... | custom-call | flops 12884901888 | bytes 62914560 | tf_op jit(solution)/shard_map/while/body/eval_jaxpr/attn_block/pallas_call | solution.py:541
  1342.7 52.5 %mlp_block.5 = (bf16[256,3072]{1,0:T(8,128)(2,1)S(1)}, bf16[12,256,256]{2,1,0:T(8,128)(2,1)}, bf16[256,3072]{1,0:T(8,128)(2,1)}) custom-call(bf16[256,3072]{1,0:T(8,128)(2,1)} %get-tuple-element.545.h1, f32[1,3072]{1,0:T(1,128)S(1)} %get-tuple-element.619.gain, bf16[256,3072]{1,0:T(8,128)(2,1)} %get-tuple-element.546.staged, ...), custom_call_target="tpu_custom_call" | custom-call | flops 38654705664 | bytes 167772160 | tf_op jit(solution)/shard_map/while/body/eval_jaxpr/mlp_block/pallas_call | solution.py:543
  1395.1 55.9 %attn_block.5 = (bf16[256,3072]{1,0:T(8,128)(2,1)}, bf16[256,3072]{1,0:T(8,128)(2,1)}, bf16[8,128,4096]{2,1,0:T(8,128)(2,1)}, bf16[8,4096,128]{2,1,0:T(8,128)(2,...) custom-call(s32[1]{0:T(128)} %bitcast.22.tick, ...), custom_call_target="tpu_custom_call", output_to_operand_aliasing={{2}: (13, {}), {3}: (14, {}), {4}: (15, {}), {5}: (16, {}),... | custom-call | flops 12884901888 | bytes 62914560 | tf_op jit(solution)/shard_map/while/body/eval_jaxpr/attn_block/pallas_call | solution.py:541
  1451.0 52.5 %mlp_block.5 = (bf16[256,3072]{1,0:T(8,128)(2,1)S(1)}, bf16[12,256,256]{2,1,0:T(8,128)(2,1)}, bf16[256,3072]{1,0:T(8,128)(2,1)}) custom-call(bf16[256,3072]{1,0:T(8,128)(2,1)} %get-tuple-element.545.h1, f32[1,3072]{1,0:T(1,128)S(1)} %get-tuple-element.619.gain, bf16[256,3072]{1,0:T(8,128)(2,1)} %get-tuple-element.546.staged, ...), custom_call_target="tpu_custom_call" | custom-call | flops 38654705664 | bytes 167772160 | tf_op jit(solution)/shard_map/while/body/eval_jaxpr/mlp_block/pallas_call | solution.py:543
  1503.5 55.8 %attn_block.5 = (bf16[256,3072]{1,0:T(8,128)(2,1)}, bf16[256,3072]{1,0:T(8,128)(2,1)}, bf16[8,128,4096]{2,1,0:T(8,128)(2,1)}, bf16[8,4096,128]{2,1,0:T(8,128)(2,...) custom-call(s32[1]{0:T(128)} %bitcast.22.tick, ...), custom_call_target="tpu_custom_call", output_to_operand_aliasing={{2}: (13, {}), {3}: (14, {}), {4}: (15, {}), {5}: (16, {}),... | custom-call | flops 12884901888 | bytes 62914560 | tf_op jit(solution)/shard_map/while/body/eval_jaxpr/attn_block/pallas_call | solution.py:541
  1559.3 52.6 %mlp_block.5 = (bf16[256,3072]{1,0:T(8,128)(2,1)S(1)}, bf16[12,256,256]{2,1,0:T(8,128)(2,1)}, bf16[256,3072]{1,0:T(8,128)(2,1)}) custom-call(bf16[256,3072]{1,0:T(8,128)(2,1)} %get-tuple-element.545.h1, f32[1,3072]{1,0:T(1,128)S(1)} %get-tuple-element.619.gain, bf16[256,3072]{1,0:T(8,128)(2,1)} %get-tuple-element.546.staged, ...), custom_call_target="tpu_custom_call" | custom-call | flops 38654705664 | bytes 167772160 | tf_op jit(solution)/shard_map/while/body/eval_jaxpr/mlp_block/pallas_call | solution.py:543
  1611.9 55.8 %attn_block.5 = (bf16[256,3072]{1,0:T(8,128)(2,1)}, bf16[256,3072]{1,0:T(8,128)(2,1)}, bf16[8,128,4096]{2,1,0:T(8,128)(2,1)}, bf16[8,4096,128]{2,1,0:T(8,128)(2,...) custom-call(s32[1]{0:T(128)} %bitcast.22.tick, ...), custom_call_target="tpu_custom_call", output_to_operand_aliasing={{2}: (13, {}), {3}: (14, {}), {4}: (15, {}), {5}: (16, {}),... | custom-call | flops 12884901888 | bytes 62914560 | tf_op jit(solution)/shard_map/while/body/eval_jaxpr/attn_block/pallas_call | solution.py:541
  1667.7 52.6 %mlp_block.5 = (bf16[256,3072]{1,0:T(8,128)(2,1)S(1)}, bf16[12,256,256]{2,1,0:T(8,128)(2,1)}, bf16[256,3072]{1,0:T(8,128)(2,1)}) custom-call(bf16[256,3072]{1,0:T(8,128)(2,1)} %get-tuple-element.545.h1, f32[1,3072]{1,0:T(1,128)S(1)} %get-tuple-element.619.gain, bf16[256,3072]{1,0:T(8,128)(2,1)} %get-tuple-element.546.staged, ...), custom_call_target="tpu_custom_call" | custom-call | flops 38654705664 | bytes 167772160 | tf_op jit(solution)/shard_map/while/body/eval_jaxpr/mlp_block/pallas_call | solution.py:543
  1720.3 55.8 %attn_block.5 = (bf16[256,3072]{1,0:T(8,128)(2,1)}, bf16[256,3072]{1,0:T(8,128)(2,1)}, bf16[8,128,4096]{2,1,0:T(8,128)(2,1)}, bf16[8,4096,128]{2,1,0:T(8,128)(2,...) custom-call(s32[1]{0:T(128)} %bitcast.22.tick, ...), custom_call_target="tpu_custom_call", output_to_operand_aliasing={{2}: (13, {}), {3}: (14, {}), {4}: (15, {}), {5}: (16, {}),... | custom-call | flops 12884901888 | bytes 62914560 | tf_op jit(solution)/shard_map/while/body/eval_jaxpr/attn_block/pallas_call | solution.py:541
  1776.1 52.6 %mlp_block.5 = (bf16[256,3072]{1,0:T(8,128)(2,1)S(1)}, bf16[12,256,256]{2,1,0:T(8,128)(2,1)}, bf16[256,3072]{1,0:T(8,128)(2,1)}) custom-call(bf16[256,3072]{1,0:T(8,128)(2,1)} %get-tuple-element.545.h1, f32[1,3072]{1,0:T(1,128)S(1)} %get-tuple-element.619.gain, bf16[256,3072]{1,0:T(8,128)(2,1)} %get-tuple-element.546.staged, ...), custom_call_target="tpu_custom_call" | custom-call | flops 38654705664 | bytes 167772160 | tf_op jit(solution)/shard_map/while/body/eval_jaxpr/mlp_block/pallas_call | solution.py:543
  1828.8 55.8 %attn_block.5 = (bf16[256,3072]{1,0:T(8,128)(2,1)}, bf16[256,3072]{1,0:T(8,128)(2,1)}, bf16[8,128,4096]{2,1,0:T(8,128)(2,1)}, bf16[8,4096,128]{2,1,0:T(8,128)(2,...) custom-call(s32[1]{0:T(128)} %bitcast.22.tick, ...), custom_call_target="tpu_custom_call", output_to_operand_aliasing={{2}: (13, {}), {3}: (14, {}), {4}: (15, {}), {5}: (16, {}),... | custom-call | flops 12884901888 | bytes 62914560 | tf_op jit(solution)/shard_map/while/body/eval_jaxpr/attn_block/pallas_call | solution.py:541
  1884.6 49.0 %mlp_block.5 = (bf16[256,3072]{1,0:T(8,128)(2,1)S(1)}, bf16[12,256,256]{2,1,0:T(8,128)(2,1)}, bf16[256,3072]{1,0:T(8,128)(2,1)}) custom-call(bf16[256,3072]{1,0:T(8,128)(2,1)} %get-tuple-element.545.h1, f32[1,3072]{1,0:T(1,128)S(1)} %get-tuple-element.619.gain, bf16[256,3072]{1,0:T(8,128)(2,1)} %get-tuple-element.546.staged, ...), custom_call_target="tpu_custom_call" | custom-call | flops 38654705664 | bytes 167772160 | tf_op jit(solution)/shard_map/while/body/eval_jaxpr/mlp_block/pallas_call | solution.py:543
  (35 shorter events, 192.4 us)
Async XLA Ops:
  1.4 10.8 copy-start.1
  8.9 4.3 copy-start
  8.9 12.1 slice-start
  8.9 12.1 slice-start.1
  13.2 7.8 slice-start.2
  13.2 8.3 slice-start.3
  13.2 10.1 slice-start.4
  23.2 12.9 copy-start.2
  23.2 12.9 copy-start.3
